TPU v7x, 512 devices: a whole 4x4x16 slice. The times are simulated.
512 devices in a mesh: phase: 8 (over y, core), wide: 64 (over x, z).
Axes of the slice: x: 4, y: 4, z: 16, core: 2. Of those that a mesh axis runs over, the one named last changes fastest.
Arguments:
- image: bfloat16 [16, 256, 16384], P(None, None, 'wide'), may hold values from -6 to 6
- conv_weight: bfloat16 [8, 256, 2304], P('phase'), may hold values from -0.09375 to 0.09375
- class_weight: bfloat16 [11, 256], replicated, may hold values from -0.375 to 0.375
- point_feats: float32 [16, 4, 16384], P('phase', None, 'wide'), may hold values from -6 to 6
- pixel_index: int32 [16, 16384], P('phase', 'wide'), may hold values from 0 to 16383
- pillar_index: int32 [16, 16384], P('phase', 'wide'), may hold values from 0 to 8191
- point_counts: int32 [16, 64], P('phase', 'wide'), may hold values from 64 to 256, as said below
- pillar_weight: float32 [64, 15], replicated, may hold values from -1.5 to 1.5
- bev_weight: bfloat16 [576, 384], replicated, may hold values from -0.25 to 0.25
- head_weight: bfloat16 [384, 20], replicated, may hold values from -0.3125 to 0.3125
Outputs:
- detections: float32 [16, 8192, 20], P('phase', 'wide')
- scores: float32 [16, 11, 16384], P('phase', None, 'wide')
Inputs may be any that keep to these rules, and one draw needn't show every extreme that they name: `point_counts`: in every frame some index of wide has all 256 slots live; slots at or past the count are padding.
All inputs are finite; a program needn't handle non-finite values.
Results may differ from a plain program's by a relative error of at most 0.01.
Values may be sent and summed in bfloat16 or wider, within the bound.
A program may use at most 64 MiB of HBM per device.

v0:
```python
import jax
import jax.numpy as jnp
from jax import lax
from jax.sharding import Mesh
from jax.sharding import PartitionSpec as P

PIL = 64
HEAD = 384
IMG_W = 64
BEV_W = 128
CELLS_DEV = 128
WIDE = ("wide_0", "wide_1")


def padded_2(value, sides, width):
    for axis, dim in sides:
        devices, length = (lax.axis_size(axis), value.shape[dim])
        up = [(i, (i + 1) % devices) for i in range(devices - 1)]
        down = [(j, i) for i, j in up]
        last = lax.slice_in_dim(value, length - width, length, axis=dim)
        first = lax.slice_in_dim(value, 0, width, axis=dim)
        before = lax.ppermute(last, axis, up)
        after = lax.ppermute(first, axis, down)
        value = jnp.concatenate([before, value, after], axis=dim)
    return value


def joined_along(parts, dim):
    dims = list(parts.shape[1:])
    dims[dim] *= parts.shape[0]
    return jnp.moveaxis(parts, 0, dim).reshape(dims)


def copy_for_each(value, axis):
    devices = lax.axis_size(axis)
    return lax.all_to_all(
        jnp.broadcast_to(value[None], (devices, *value.shape)), axis, 0, 0, tiled=True
    )


def gather_directly(value, axis, dim):
    return joined_along(copy_for_each(value, axis), dim)


def whole_of(value, axes, dim):
    filled = value
    for number in range(len(axes) - 1, -1, -1):
        filled = lax.all_gather(filled, axes[number], axis=dim, tiled=True)
    return filled


def image_layer(activation, weight):
    length = activation.shape[2]
    padded = padded_2(activation, ((WIDE, 2),), IMG_W)
    extended = jnp.pad(padded, ((0, 0), (0, 0), (1, 1)))
    column = jnp.arange(length, dtype=jnp.int32) % IMG_W
    sections = []
    for row_step in range(3):
        for col_step in range(3):
            offset = row_step * IMG_W + col_step
            section = lax.slice_in_dim(extended, offset, offset + length, axis=2)
            inside = (column + col_step - 1 >= 0) & (column + col_step - 1 < IMG_W)
            sections.append(jnp.where(inside[None, None, :], section, jnp.zeros_like(section)))
    stacked = jnp.concatenate(sections, axis=1)
    summed = jnp.einsum("ok,fkp->fop", weight, stacked, preferred_element_type=jnp.float32)
    return (activation.astype(jnp.float32) + jax.nn.relu(summed)).astype(jnp.bfloat16)


def bev_layer(grid, bev_weight, own_frames):
    padded = padded_2(grid, ((WIDE, 0),), BEV_W)
    extended = jnp.pad(padded, ((1, 1), (0, 0)))
    column = jnp.arange(CELLS_DEV, dtype=jnp.int32) % BEV_W
    sections = []
    for row_step in range(3):
        for col_step in range(3):
            offset = row_step * BEV_W + col_step
            section = lax.slice_in_dim(extended, offset, offset + CELLS_DEV, axis=0)
            inside = (column + col_step - 1 >= 0) & (column + col_step - 1 < BEV_W)
            sections.append(jnp.where(inside[:, None], section, jnp.zeros_like(section)))
    stacked = jnp.stack(sections, axis=1).reshape(CELLS_DEV, 9, own_frames, PIL)
    summed = jnp.einsum(
        "ctfj,tjo->fco",
        stacked,
        bev_weight.reshape(9, PIL, HEAD),
        preferred_element_type=jnp.float32,
    )
    return jax.nn.relu(summed).astype(jnp.bfloat16)


def local(
    image,
    conv_weight,
    class_weight,
    point_feats,
    pixel_index,
    pillar_index,
    point_counts,
    pillar_weight,
    bev_weight,
    head_weight,
):
    phase_now = lax.axis_index("phase")
    phases = lax.axis_size("phase")
    own_frames = point_feats.shape[0]
    weights = lax.all_gather(conv_weight, "phase", axis=0, tiled=True)
    start_maps = lax.dynamic_slice_in_dim(image, phase_now * own_frames, own_frames, 0)

    def layer_step(layer, activation):
        return image_layer(activation, lax.dynamic_index_in_dim(weights, layer, 0, keepdims=False))

    own_maps = lax.fori_loop(0, phases, layer_step, start_maps)
    scores = jnp.einsum("kc,fcp->fkp", class_weight, own_maps, preferred_element_type=jnp.float32)
    logits = scores.astype(jnp.bfloat16)
    section = gather_directly(logits, WIDE, 2)
    extent = section.shape[2]
    onehot = (pixel_index[:, None, :] == jnp.arange(extent, dtype=jnp.int32)[None, :, None]).astype(
        jnp.bfloat16
    )
    painted = jnp.einsum("fkn,fnp->fkp", section, onehot, preferred_element_type=jnp.float32)
    features = jnp.concatenate([point_feats, jax.nn.sigmoid(painted)], axis=1)
    hidden = jax.nn.relu(
        jnp.einsum("jd,fdp->fjp", pillar_weight, features, precision=lax.Precision.HIGHEST)
    )
    positions = jnp.arange(pixel_index.shape[1], dtype=jnp.int32)
    is_live = positions[None, :] < point_counts
    hidden = jnp.where(is_live[:, None, :], hidden, 0.0).astype(jnp.bfloat16)
    own_first = lax.axis_index(WIDE) * CELLS_DEV
    part_hidden = whole_of(hidden, ("wide_1", "wide_0"), 2)
    part_index = whole_of(pillar_index[:, None, :], ("wide_1", "wide_0"), 2)
    onehot = (
        part_index[:, 0, :, None] - own_first
        == jnp.arange(CELLS_DEV, dtype=jnp.int32)[None, None, :]
    ).astype(jnp.bfloat16)
    partial_sum = jnp.einsum(
        "fjp,fpc->cfj", part_hidden, onehot, preferred_element_type=jnp.float32
    )
    pooled = partial_sum.reshape(CELLS_DEV, own_frames * PIL)
    grid = pooled.astype(jnp.bfloat16)
    feature = bev_layer(grid, bev_weight, own_frames)
    detections = jnp.einsum("fco,or->fcr", feature, head_weight, preferred_element_type=jnp.float32)
    return (detections, scores)


def solution(mesh):
    finer = Mesh(mesh.devices.reshape(mesh.shape["phase"], 4, 16), ("phase", "wide_0", "wide_1"))
    placed = (
        P(None, None, WIDE),
        P("phase", None, None),
        P(),
        P("phase", None, WIDE),
        P("phase", WIDE),
        P("phase", WIDE),
        P("phase", WIDE),
        P(),
        P(),
        P(),
    )
    return jax.shard_map(
        local,
        mesh=finer,
        in_specs=placed,
        out_specs=(P("phase", WIDE, None), P("phase", None, WIDE)),
        check_vma=False,
    )
```

profile of v0, /device:TPU:6, one launch (start us, length us, event | category | flops | bytes accessed | tf_op | source)
XLA Modules:
  0.0 344.1 jit_solution(6971880708646652760)
XLA Ops:
  8.9 67.4 %all-gather.5.cloned.1.call-done = bf16[8,256,2304]{2,1,0:T(8,128)(2,1)} async-done(((bf16[1,256,2304]{2,1,0:T(8,128)(2,1)}), bf16[8,256,2304]{2,1,0:T(8,128)(2,1)}) %all-gather.5.cloned.1.call-update) | async-done | bytes 9437200 | tf_op jit(solution)/shard_map/all_gather | solution.py:105
  76.3 112.8 %while.18 = (s32[]{:T(128)}, bf16[2,256,256]{1,2,0:T(8,128)(2,1)S(1)}, bf16[8,256,2304]{2,1,0:T(8,128)(2,1)}, s32[]{:T(128)}) while((s32[]{:T(128)}, bf16[2,256,256]{1,2,0:T(8,128)(2,1)S(1)}, bf16[8,256,2304]{2,1,0:T(8,128)(2,1)}, s32[]{:T(128)}) %tuple.72), condition=%wide.region_1.2_spmd, body=%wide.region_0.1_spmd.sunk | while | flops 608062720 | bytes 11410577 | solution.py:111
  76.3 6.2 %collective-permute-start = (bf16[2,256,64]{1,2,0:T(8,128)(2,1)S(1)}, bf16[2,256,64]{1,2,0:T(8,128)(2,1)S(1)}, u32[]{:S(2)}, u32[]{:S(2)}) collective-permute-start(bf16[2,256,64]{1,2,0:T(8,128)(2,1)S(1)} %get-tuple-element.195), channel_id=1, source_target_pairs={{1,0},{2,1},{3,2},{4,3},{5,4},{6,5},{7,6},{8,7},{9,8},{10,9},{11,1... | collective-permute-start | bytes 196616 | tf_op jit(solution)/shard_map/while/body/eval_jaxpr/ppermute | solution.py:23
  84.5 6.3 %collective-permute-done.1 = bf16[2,256,64]{1,2,0:T(8,128)(2,1)S(1)} collective-permute-done((bf16[2,256,64]{1,2,0:T(8,128)(2,1)S(1)}, bf16[2,256,64]{1,2,0:T(8,128)(2,1)S(1)}, u32[]{:S(2)}, u32[]{:S(2)}) %collective-permute-start.1) | collective-permute-done | bytes 65568 | tf_op jit(solution)/shard_map/while/body/eval_jaxpr/ppermute | solution.py:22
  96.1 3.9 %collective-permute-start.1 = (bf16[2,256,64]{1,2,0:T(8,128)(2,1)S(1)}, bf16[2,256,64]{1,2,0:T(8,128)(2,1)S(1)}, u32[]{:S(2)}, u32[]{:S(2)}) collective-permute-start(bf16[2,256,64]{1,2,0:T(8,128)(2,1)S(1)} %get-tuple-element.196), channel_id=1, source_target_pairs={{0,1},{1,2},{2,3},{3,4},{4,5},{5,6},{6,7},{7,8},{8,9},{9,10},{10,1... | collective-permute-start | bytes 196616 | tf_op jit(solution)/shard_map/while/body/eval_jaxpr/ppermute | solution.py:22
  100.1 4.3 %collective-permute-done.1 = bf16[2,256,64]{1,2,0:T(8,128)(2,1)S(1)} collective-permute-done((bf16[2,256,64]{1,2,0:T(8,128)(2,1)S(1)}, bf16[2,256,64]{1,2,0:T(8,128)(2,1)S(1)}, u32[]{:S(2)}, u32[]{:S(2)}) %collective-permute-start.1) | collective-permute-done | bytes 65568 | tf_op jit(solution)/shard_map/while/body/eval_jaxpr/ppermute | solution.py:22
  109.7 3.9 %collective-permute-start.1 = (bf16[2,256,64]{1,2,0:T(8,128)(2,1)S(1)}, bf16[2,256,64]{1,2,0:T(8,128)(2,1)S(1)}, u32[]{:S(2)}, u32[]{:S(2)}) collective-permute-start(bf16[2,256,64]{1,2,0:T(8,128)(2,1)S(1)} %get-tuple-element.196), channel_id=1, source_target_pairs={{0,1},{1,2},{2,3},{3,4},{4,5},{5,6},{6,7},{7,8},{8,9},{9,10},{10,1... | collective-permute-start | bytes 196616 | tf_op jit(solution)/shard_map/while/body/eval_jaxpr/ppermute | solution.py:22
  113.7 4.3 %collective-permute-done.1 = bf16[2,256,64]{1,2,0:T(8,128)(2,1)S(1)} collective-permute-done((bf16[2,256,64]{1,2,0:T(8,128)(2,1)S(1)}, bf16[2,256,64]{1,2,0:T(8,128)(2,1)S(1)}, u32[]{:S(2)}, u32[]{:S(2)}) %collective-permute-start.1) | collective-permute-done | bytes 65568 | tf_op jit(solution)/shard_map/while/body/eval_jaxpr/ppermute | solution.py:22
  119.2 2.1 fusion.91
  123.3 3.9 %collective-permute-start.1 = (bf16[2,256,64]{1,2,0:T(8,128)(2,1)S(1)}, bf16[2,256,64]{1,2,0:T(8,128)(2,1)S(1)}, u32[]{:S(2)}, u32[]{:S(2)}) collective-permute-start(bf16[2,256,64]{1,2,0:T(8,128)(2,1)S(1)} %get-tuple-element.196), channel_id=1, source_target_pairs={{0,1},{1,2},{2,3},{3,4},{4,5},{5,6},{6,7},{7,8},{8,9},{9,10},{10,1... | collective-permute-start | bytes 196616 | tf_op jit(solution)/shard_map/while/body/eval_jaxpr/ppermute | solution.py:22
  127.2 4.3 %collective-permute-done.1 = bf16[2,256,64]{1,2,0:T(8,128)(2,1)S(1)} collective-permute-done((bf16[2,256,64]{1,2,0:T(8,128)(2,1)S(1)}, bf16[2,256,64]{1,2,0:T(8,128)(2,1)S(1)}, u32[]{:S(2)}, u32[]{:S(2)}) %collective-permute-start.1) | collective-permute-done | bytes 65568 | tf_op jit(solution)/shard_map/while/body/eval_jaxpr/ppermute | solution.py:22
  132.8 2.1 fusion.91
  136.8 3.9 %collective-permute-start.1 = (bf16[2,256,64]{1,2,0:T(8,128)(2,1)S(1)}, bf16[2,256,64]{1,2,0:T(8,128)(2,1)S(1)}, u32[]{:S(2)}, u32[]{:S(2)}) collective-permute-start(bf16[2,256,64]{1,2,0:T(8,128)(2,1)S(1)} %get-tuple-element.196), channel_id=1, source_target_pairs={{0,1},{1,2},{2,3},{3,4},{4,5},{5,6},{6,7},{7,8},{8,9},{9,10},{10,1... | collective-permute-start | bytes 196616 | tf_op jit(solution)/shard_map/while/body/eval_jaxpr/ppermute | solution.py:22
  140.8 4.3 %collective-permute-done.1 = bf16[2,256,64]{1,2,0:T(8,128)(2,1)S(1)} collective-permute-done((bf16[2,256,64]{1,2,0:T(8,128)(2,1)S(1)}, bf16[2,256,64]{1,2,0:T(8,128)(2,1)S(1)}, u32[]{:S(2)}, u32[]{:S(2)}) %collective-permute-start.1) | collective-permute-done | bytes 65568 | tf_op jit(solution)/shard_map/while/body/eval_jaxpr/ppermute | solution.py:22
  150.4 3.9 %collective-permute-start.1 = (bf16[2,256,64]{1,2,0:T(8,128)(2,1)S(1)}, bf16[2,256,64]{1,2,0:T(8,128)(2,1)S(1)}, u32[]{:S(2)}, u32[]{:S(2)}) collective-permute-start(bf16[2,256,64]{1,2,0:T(8,128)(2,1)S(1)} %get-tuple-element.196), channel_id=1, source_target_pairs={{0,1},{1,2},{2,3},{3,4},{4,5},{5,6},{6,7},{7,8},{8,9},{9,10},{10,1... | collective-permute-start | bytes 196616 | tf_op jit(solution)/shard_map/while/body/eval_jaxpr/ppermute | solution.py:22
  154.4 4.3 %collective-permute-done.1 = bf16[2,256,64]{1,2,0:T(8,128)(2,1)S(1)} collective-permute-done((bf16[2,256,64]{1,2,0:T(8,128)(2,1)S(1)}, bf16[2,256,64]{1,2,0:T(8,128)(2,1)S(1)}, u32[]{:S(2)}, u32[]{:S(2)}) %collective-permute-start.1) | collective-permute-done | bytes 65568 | tf_op jit(solution)/shard_map/while/body/eval_jaxpr/ppermute | solution.py:22
  159.9 2.1 fusion.91
  164.0 3.9 %collective-permute-start.1 = (bf16[2,256,64]{1,2,0:T(8,128)(2,1)S(1)}, bf16[2,256,64]{1,2,0:T(8,128)(2,1)S(1)}, u32[]{:S(2)}, u32[]{:S(2)}) collective-permute-start(bf16[2,256,64]{1,2,0:T(8,128)(2,1)S(1)} %get-tuple-element.196), channel_id=1, source_target_pairs={{0,1},{1,2},{2,3},{3,4},{4,5},{5,6},{6,7},{7,8},{8,9},{9,10},{10,1... | collective-permute-start | bytes 196616 | tf_op jit(solution)/shard_map/while/body/eval_jaxpr/ppermute | solution.py:22
  167.9 4.3 %collective-permute-done.1 = bf16[2,256,64]{1,2,0:T(8,128)(2,1)S(1)} collective-permute-done((bf16[2,256,64]{1,2,0:T(8,128)(2,1)S(1)}, bf16[2,256,64]{1,2,0:T(8,128)(2,1)S(1)}, u32[]{:S(2)}, u32[]{:S(2)}) %collective-permute-start.1) | collective-permute-done | bytes 65568 | tf_op jit(solution)/shard_map/while/body/eval_jaxpr/ppermute | solution.py:22
  173.5 2.1 fusion.91
  177.5 3.9 %collective-permute-start.1 = (bf16[2,256,64]{1,2,0:T(8,128)(2,1)S(1)}, bf16[2,256,64]{1,2,0:T(8,128)(2,1)S(1)}, u32[]{:S(2)}, u32[]{:S(2)}) collective-permute-start(bf16[2,256,64]{1,2,0:T(8,128)(2,1)S(1)} %get-tuple-element.196), channel_id=1, source_target_pairs={{0,1},{1,2},{2,3},{3,4},{4,5},{5,6},{6,7},{7,8},{8,9},{9,10},{10,1... | collective-permute-start | bytes 196616 | tf_op jit(solution)/shard_map/while/body/eval_jaxpr/ppermute | solution.py:22
  181.5 4.3 %collective-permute-done.1 = bf16[2,256,64]{1,2,0:T(8,128)(2,1)S(1)} collective-permute-done((bf16[2,256,64]{1,2,0:T(8,128)(2,1)S(1)}, bf16[2,256,64]{1,2,0:T(8,128)(2,1)S(1)}, u32[]{:S(2)}, u32[]{:S(2)}) %collective-permute-start.1) | collective-permute-done | bytes 65568 | tf_op jit(solution)/shard_map/while/body/eval_jaxpr/ppermute | solution.py:22
  191.2 5.4 %all-to-all-start = ((bf16[64,2,11,256]{3,1,2,0:T(2,128)(2,1)}), bf16[64,2,11,256]{3,1,2,0:T(2,128)(2,1)S(1)}, u32[]{:S(2)}, u32[]{:S(2)}) async-start(bf16[64,2,11,256]{3,1,2,0:T(2,128)(2,1)} %broadcast_in_dim.201), calls=%async_computation | async-start | bytes 1441792 | tf_op jit(solution)/shard_map/all_to_all | solution.py:36
  196.8 29.8 %all-to-all-done = bf16[64,2,11,256]{3,1,2,0:T(2,128)(2,1)S(1)} async-done(((bf16[64,2,11,256]{3,1,2,0:T(2,128)(2,1)}), bf16[64,2,11,256]{3,1,2,0:T(2,128)(2,1)S(1)}, u32[]{:S(2)}, u32[]{:S(2)}) %all-to-all-start) | async-done | bytes 720928 | tf_op jit(solution)/shard_map/all_to_all | solution.py:36
  228.2 6.5 %fusion.35 = f32[2,11,256]{2,1,0:T(8,128)S(1)} fusion(bf16[2,11,16384]{2,1,0:T(8,128)(2,1)} %reshape.132, s32[2,256]{1,0:T(2,128)S(1)} %copy-done.7), kind=kOutput, calls=%fused_computation.59 | convolution fusion | flops 192954880 | bytes 745472 | tf_op jit(solution)/shard_map/fkn,fnp->fkp/dot_general | solution.py:119
  235.1 13.0 %all_gather.18 = bf16[2,64,1024]{2,1,0:T(8,128)(2,1)} all-gather(bf16[2,64,256]{2,1,0:T(8,128)(2,1)S(1)} %fusion.30), channel_id=1, replica_groups=mesh['phase'=8,'wide_0'=4,'wide_1'=16] {'wide_0'}, dimensions={2}, use_global_device_ids=true | all-gather | bytes 327680 | tf_op jit(solution)/shard_map/all_gather | solution.py:48
  248.1 10.2 %all-gather = s32[2,1024]{1,0:T(2,128)S(1)} all-gather(s32[2,256]{1,0:T(2,128)S(1)} %copy-done.4), channel_id=2, replica_groups=mesh['phase'=8,'wide_0'=4,'wide_1'=16] {'wide_0'}, dimensions={1}, use_global_device_ids=true | all-gather | bytes 10240 | tf_op jit(solution)/shard_map/all_gather | solution.py:48
  258.3 29.0 %all-gather.1 = s32[2,16384]{1,0:T(2,128)S(1)} all-gather(s32[2,1024]{1,0:T(2,128)S(1)} %all-gather), channel_id=3, replica_groups=mesh['phase'=8,'wide_0'=4,'wide_1'=16] {'wide_1'}, dimensions={1}, use_global_device_ids=true | all-gather | bytes 139264 | tf_op jit(solution)/shard_map/all_gather | solution.py:48
  287.4 31.9 %all-gather.7.cloned.1.call-done = bf16[2,64,16384]{2,1,0:T(8,128)(2,1)} async-done(((bf16[2,64,1024]{2,1,0:T(8,128)(2,1)}), bf16[2,64,16384]{2,1,0:T(8,128)(2,1)}) %all-gather.7.cloned.1.call-update) | async-done | bytes 4194320 | tf_op jit(solution)/shard_map/all_gather | solution.py:48
  319.3 6.7 %fusion.31 = bf16[2,128,64]{1,2,0:T(8,128)(2,1)S(1)} fusion(bf16[2,64,16384]{2,1,0:T(8,128)(2,1)} %all-gather.7.cloned.1.call-done, s32[2,16384]{1,0:T(2,128)S(1)} %broadcast_subtract_fusion), kind=kOutput, calls=%fused_computation.55 | convolution fusion | flops 541081600 | bytes 4358144 | tf_op jit(solution)/shard_map/fjp,fpc->cfj/dot_general | solution.py:134
  326.1 2.6 collective-permute-start.2
  328.6 5.4 %collective-permute-start.3 = (bf16[128,128]{0,1:T(8,128)(2,1)S(1)}, bf16[128,128]{0,1:T(8,128)(2,1)S(1)}, u32[]{:S(2)}, u32[]{:S(2)}) collective-permute-start(bf16[128,128]{0,1:T(8,128)(2,1)S(1)} %bitcast.77), channel_id=1, source_target_pairs={{1,0},{2,1},{3,2},{4,3},{5,4},{6,5},{7,6},{8,7},{9,8},{10,9},{11,1... | collective-permute-start | bytes 98312 | tf_op jit(solution)/shard_map/ppermute | solution.py:23
  (205 shorter events, 42.1 us)
Async XLA Ops:
  7.2 1.6 copy-start
  7.2 69.1 %all-gather.5.cloned.1.call-start = ((), (), s32[]{:S(2)}) async-start(), calls=%async_computation.1 | async-start | bytes 10616832 | tf_op jit(solution)/shard_map/all_gather | solution.py:105
  76.3 112.9 %copy-start.3 = (bf16[11,256]{1,0:T(8,128)(2,1)S(1)}, bf16[11,256]{1,0:T(8,128)(2,1)}, u32[]{:S(2)}) copy-start(bf16[11,256]{1,0:T(8,128)(2,1)} %param.14) | copy-start | bytes 16900
  76.3 14.5 %collective-permute-start = (bf16[2,256,64]{1,2,0:T(8,128)(2,1)S(1)}, bf16[2,256,64]{1,2,0:T(8,128)(2,1)S(1)}, u32[]{:S(2)}, u32[]{:S(2)}) collective-permute-start(bf16[2,256,64]{1,2,0:T(8,128)(2,1)S(1)} %get-tuple-element.195), channel_id=1, source_target_pairs={{1,0},{2,1},{3,2},{4,3},{5,4},{6,5},{7,6},{8,7},{9,8},{10,9},{11,1... | collective-permute-start | bytes 196616 | tf_op jit(solution)/shard_map/while/body/eval_jaxpr/ppermute | solution.py:23
  82.6 8.3 %collective-permute-start.1 = (bf16[2,256,64]{1,2,0:T(8,128)(2,1)S(1)}, bf16[2,256,64]{1,2,0:T(8,128)(2,1)S(1)}, u32[]{:S(2)}, u32[]{:S(2)}) collective-permute-start(bf16[2,256,64]{1,2,0:T(8,128)(2,1)S(1)} %get-tuple-element.196), channel_id=1, source_target_pairs={{0,1},{1,2},{2,3},{3,4},{4,5},{5,6},{6,7},{7,8},{8,9},{9,10},{10,1... | collective-permute-start | bytes 196616 | tf_op jit(solution)/shard_map/while/body/eval_jaxpr/ppermute | solution.py:22
  94.2 10.2 %collective-permute-start = (bf16[2,256,64]{1,2,0:T(8,128)(2,1)S(1)}, bf16[2,256,64]{1,2,0:T(8,128)(2,1)S(1)}, u32[]{:S(2)}, u32[]{:S(2)}) collective-permute-start(bf16[2,256,64]{1,2,0:T(8,128)(2,1)S(1)} %get-tuple-element.195), channel_id=1, source_target_pairs={{1,0},{2,1},{3,2},{4,3},{5,4},{6,5},{7,6},{8,7},{9,8},{10,9},{11,1... | collective-permute-start | bytes 196616 | tf_op jit(solution)/shard_map/while/body/eval_jaxpr/ppermute | solution.py:23
  96.1 8.3 %collective-permute-start.1 = (bf16[2,256,64]{1,2,0:T(8,128)(2,1)S(1)}, bf16[2,256,64]{1,2,0:T(8,128)(2,1)S(1)}, u32[]{:S(2)}, u32[]{:S(2)}) collective-permute-start(bf16[2,256,64]{1,2,0:T(8,128)(2,1)S(1)} %get-tuple-element.196), channel_id=1, source_target_pairs={{0,1},{1,2},{2,3},{3,4},{4,5},{5,6},{6,7},{7,8},{8,9},{9,10},{10,1... | collective-permute-start | bytes 196616 | tf_op jit(solution)/shard_map/while/body/eval_jaxpr/ppermute | solution.py:22
  107.8 10.2 %collective-permute-start = (bf16[2,256,64]{1,2,0:T(8,128)(2,1)S(1)}, bf16[2,256,64]{1,2,0:T(8,128)(2,1)S(1)}, u32[]{:S(2)}, u32[]{:S(2)}) collective-permute-start(bf16[2,256,64]{1,2,0:T(8,128)(2,1)S(1)} %get-tuple-element.195), channel_id=1, source_target_pairs={{1,0},{2,1},{3,2},{4,3},{5,4},{6,5},{7,6},{8,7},{9,8},{10,9},{11,1... | collective-permute-start | bytes 196616 | tf_op jit(solution)/shard_map/while/body/eval_jaxpr/ppermute | solution.py:23
  109.7 8.3 %collective-permute-start.1 = (bf16[2,256,64]{1,2,0:T(8,128)(2,1)S(1)}, bf16[2,256,64]{1,2,0:T(8,128)(2,1)S(1)}, u32[]{:S(2)}, u32[]{:S(2)}) collective-permute-start(bf16[2,256,64]{1,2,0:T(8,128)(2,1)S(1)} %get-tuple-element.196), channel_id=1, source_target_pairs={{0,1},{1,2},{2,3},{3,4},{4,5},{5,6},{6,7},{7,8},{8,9},{9,10},{10,1... | collective-permute-start | bytes 196616 | tf_op jit(solution)/shard_map/while/body/eval_jaxpr/ppermute | solution.py:22
  121.3 10.2 %collective-permute-start = (bf16[2,256,64]{1,2,0:T(8,128)(2,1)S(1)}, bf16[2,256,64]{1,2,0:T(8,128)(2,1)S(1)}, u32[]{:S(2)}, u32[]{:S(2)}) collective-permute-start(bf16[2,256,64]{1,2,0:T(8,128)(2,1)S(1)} %get-tuple-element.195), channel_id=1, source_target_pairs={{1,0},{2,1},{3,2},{4,3},{5,4},{6,5},{7,6},{8,7},{9,8},{10,9},{11,1... | collective-permute-start | bytes 196616 | tf_op jit(solution)/shard_map/while/body/eval_jaxpr/ppermute | solution.py:23
  123.3 8.3 %collective-permute-start.1 = (bf16[2,256,64]{1,2,0:T(8,128)(2,1)S(1)}, bf16[2,256,64]{1,2,0:T(8,128)(2,1)S(1)}, u32[]{:S(2)}, u32[]{:S(2)}) collective-permute-start(bf16[2,256,64]{1,2,0:T(8,128)(2,1)S(1)} %get-tuple-element.196), channel_id=1, source_target_pairs={{0,1},{1,2},{2,3},{3,4},{4,5},{5,6},{6,7},{7,8},{8,9},{9,10},{10,1... | collective-permute-start | bytes 196616 | tf_op jit(solution)/shard_map/while/body/eval_jaxpr/ppermute | solution.py:22
  134.9 10.2 %collective-permute-start = (bf16[2,256,64]{1,2,0:T(8,128)(2,1)S(1)}, bf16[2,256,64]{1,2,0:T(8,128)(2,1)S(1)}, u32[]{:S(2)}, u32[]{:S(2)}) collective-permute-start(bf16[2,256,64]{1,2,0:T(8,128)(2,1)S(1)} %get-tuple-element.195), channel_id=1, source_target_pairs={{1,0},{2,1},{3,2},{4,3},{5,4},{6,5},{7,6},{8,7},{9,8},{10,9},{11,1... | collective-permute-start | bytes 196616 | tf_op jit(solution)/shard_map/while/body/eval_jaxpr/ppermute | solution.py:23
  136.8 8.3 %collective-permute-start.1 = (bf16[2,256,64]{1,2,0:T(8,128)(2,1)S(1)}, bf16[2,256,64]{1,2,0:T(8,128)(2,1)S(1)}, u32[]{:S(2)}, u32[]{:S(2)}) collective-permute-start(bf16[2,256,64]{1,2,0:T(8,128)(2,1)S(1)} %get-tuple-element.196), channel_id=1, source_target_pairs={{0,1},{1,2},{2,3},{3,4},{4,5},{5,6},{6,7},{7,8},{8,9},{9,10},{10,1... | collective-permute-start | bytes 196616 | tf_op jit(solution)/shard_map/while/body/eval_jaxpr/ppermute | solution.py:22
  148.5 10.2 %collective-permute-start = (bf16[2,256,64]{1,2,0:T(8,128)(2,1)S(1)}, bf16[2,256,64]{1,2,0:T(8,128)(2,1)S(1)}, u32[]{:S(2)}, u32[]{:S(2)}) collective-permute-start(bf16[2,256,64]{1,2,0:T(8,128)(2,1)S(1)} %get-tuple-element.195), channel_id=1, source_target_pairs={{1,0},{2,1},{3,2},{4,3},{5,4},{6,5},{7,6},{8,7},{9,8},{10,9},{11,1... | collective-permute-start | bytes 196616 | tf_op jit(solution)/shard_map/while/body/eval_jaxpr/ppermute | solution.py:23
  150.4 8.3 %collective-permute-start.1 = (bf16[2,256,64]{1,2,0:T(8,128)(2,1)S(1)}, bf16[2,256,64]{1,2,0:T(8,128)(2,1)S(1)}, u32[]{:S(2)}, u32[]{:S(2)}) collective-permute-start(bf16[2,256,64]{1,2,0:T(8,128)(2,1)S(1)} %get-tuple-element.196), channel_id=1, source_target_pairs={{0,1},{1,2},{2,3},{3,4},{4,5},{5,6},{6,7},{7,8},{8,9},{9,10},{10,1... | collective-permute-start | bytes 196616 | tf_op jit(solution)/shard_map/while/body/eval_jaxpr/ppermute | solution.py:22
  162.1 10.2 %collective-permute-start = (bf16[2,256,64]{1,2,0:T(8,128)(2,1)S(1)}, bf16[2,256,64]{1,2,0:T(8,128)(2,1)S(1)}, u32[]{:S(2)}, u32[]{:S(2)}) collective-permute-start(bf16[2,256,64]{1,2,0:T(8,128)(2,1)S(1)} %get-tuple-element.195), channel_id=1, source_target_pairs={{1,0},{2,1},{3,2},{4,3},{5,4},{6,5},{7,6},{8,7},{9,8},{10,9},{11,1... | collective-permute-start | bytes 196616 | tf_op jit(solution)/shard_map/while/body/eval_jaxpr/ppermute | solution.py:23
  164.0 8.3 %collective-permute-start.1 = (bf16[2,256,64]{1,2,0:T(8,128)(2,1)S(1)}, bf16[2,256,64]{1,2,0:T(8,128)(2,1)S(1)}, u32[]{:S(2)}, u32[]{:S(2)}) collective-permute-start(bf16[2,256,64]{1,2,0:T(8,128)(2,1)S(1)} %get-tuple-element.196), channel_id=1, source_target_pairs={{0,1},{1,2},{2,3},{3,4},{4,5},{5,6},{6,7},{7,8},{8,9},{9,10},{10,1... | collective-permute-start | bytes 196616 | tf_op jit(solution)/shard_map/while/body/eval_jaxpr/ppermute | solution.py:22
  175.6 10.2 %collective-permute-start = (bf16[2,256,64]{1,2,0:T(8,128)(2,1)S(1)}, bf16[2,256,64]{1,2,0:T(8,128)(2,1)S(1)}, u32[]{:S(2)}, u32[]{:S(2)}) collective-permute-start(bf16[2,256,64]{1,2,0:T(8,128)(2,1)S(1)} %get-tuple-element.195), channel_id=1, source_target_pairs={{1,0},{2,1},{3,2},{4,3},{5,4},{6,5},{7,6},{8,7},{9,8},{10,9},{11,1... | collective-permute-start | bytes 196616 | tf_op jit(solution)/shard_map/while/body/eval_jaxpr/ppermute | solution.py:23
  177.5 8.3 %collective-permute-start.1 = (bf16[2,256,64]{1,2,0:T(8,128)(2,1)S(1)}, bf16[2,256,64]{1,2,0:T(8,128)(2,1)S(1)}, u32[]{:S(2)}, u32[]{:S(2)}) collective-permute-start(bf16[2,256,64]{1,2,0:T(8,128)(2,1)S(1)} %get-tuple-element.196), channel_id=1, source_target_pairs={{0,1},{1,2},{2,3},{3,4},{4,5},{5,6},{6,7},{7,8},{8,9},{9,10},{10,1... | collective-permute-start | bytes 196616 | tf_op jit(solution)/shard_map/while/body/eval_jaxpr/ppermute | solution.py:22
  189.2 7.6 %copy-start.8 = (s32[2,1]{0,1:T(1,128)S(1)}, s32[2,1]{0,1:T(1,128)}, u32[]{:S(2)}) copy-start(s32[2,1]{0,1:T(1,128)} %param.18) | copy-start | bytes 28
  191.2 36.9 %copy-start.7 = (s32[2,256]{1,0:T(2,128)S(1)}, s32[2,256]{1,0:T(2,128)}, u32[]{:S(2)}) copy-start(s32[2,256]{1,0:T(2,128)} %param.16) | copy-start | bytes 6148
  191.2 35.3 %all-to-all-start = ((bf16[64,2,11,256]{3,1,2,0:T(2,128)(2,1)}), bf16[64,2,11,256]{3,1,2,0:T(2,128)(2,1)S(1)}, u32[]{:S(2)}, u32[]{:S(2)}) async-start(bf16[64,2,11,256]{3,1,2,0:T(2,128)(2,1)} %broadcast_in_dim.201), calls=%async_computation | async-start | bytes 1441792 | tf_op jit(solution)/shard_map/all_to_all | solution.py:36
  196.7 122.6 %all-gather.7.cloned.1.call-start = ((), (), s32[]{:S(2)}) async-start(), calls=%async_computation.2 | async-start | bytes 4456448 | tf_op jit(solution)/shard_map/all_gather | solution.py:48
  228.2 6.6 %copy-start.5 = (f32[2,4,256]{2,1,0:T(4,128)S(1)}, f32[2,4,256]{2,1,0:T(4,128)}, u32[]{:S(2)}) copy-start(f32[2,4,256]{2,1,0:T(4,128)} %param.15) | copy-start | bytes 24580
  228.2 6.6 %copy-start.6 = (f32[64,15]{0,1:T(8,128)S(1)}, f32[64,15]{0,1:T(8,128)}, u32[]{:S(2)}) copy-start(f32[64,15]{0,1:T(8,128)} %param.19) | copy-start | bytes 11524
  228.2 19.9 %copy-start.4 = (s32[2,256]{1,0:T(2,128)S(1)}, s32[2,256]{1,0:T(2,128)}, u32[]{:S(2)}) copy-start(s32[2,256]{1,0:T(2,128)} %param.17) | copy-start | bytes 6148
  287.4 48.7 %copy-start.1 = (bf16[576,384]{1,0:T(8,128)(2,1)S(1)}, bf16[576,384]{1,0:T(8,128)(2,1)}, u32[]{:S(2)}) copy-start(bf16[576,384]{1,0:T(8,128)(2,1)} %param.20) | copy-start | bytes 1327108
  287.4 48.7 %copy-start.2 = (bf16[384,20]{0,1:T(8,128)(2,1)S(1)}, bf16[384,20]{0,1:T(8,128)(2,1)}, u32[]{:S(2)}) copy-start(bf16[384,20]{0,1:T(8,128)(2,1)} %param.21) | copy-start | bytes 46084
  326.1 8.0 %collective-permute-start.2 = (bf16[128,128]{0,1:T(8,128)(2,1)S(1)}, bf16[128,128]{0,1:T(8,128)(2,1)S(1)}, u32[]{:S(2)}, u32[]{:S(2)}) collective-permute-start(bf16[128,128]{0,1:T(8,128)(2,1)S(1)} %bitcast.76), channel_id=1, source_target_pairs={{0,1},{1,2},{2,3},{3,4},{4,5},{5,6},{6,7},{7,8},{8,9},{9,10},{10,1... | collective-permute-start | bytes 98312 | tf_op jit(solution)/shard_map/ppermute | solution.py:22
  328.6 7.0 %collective-permute-start.3 = (bf16[128,128]{0,1:T(8,128)(2,1)S(1)}, bf16[128,128]{0,1:T(8,128)(2,1)S(1)}, u32[]{:S(2)}, u32[]{:S(2)}) collective-permute-start(bf16[128,128]{0,1:T(8,128)(2,1)S(1)} %bitcast.77), channel_id=1, source_target_pairs={{1,0},{2,1},{3,2},{4,3},{5,4},{6,5},{7,6},{8,7},{9,8},{10,9},{11,1... | collective-permute-start | bytes 98312 | tf_op jit(solution)/shard_map/ppermute | solution.py:23
Sparse Core Ops, SparseCore 0:
  10.1 66.1 all-gather.4
  248.2 71.0 all-gather.6
where the time goes:
time: 345 us; the launch traced here: 344 us
  waiting for transfers between devices  168 us (49%)
  starting transfers between devices  62.5 us (18%)
  blocking collectives  52.2 us (15%)
  matrix products  31 us (9%)
  between operations  14.3 us (4%)
  other arithmetic  10.2 us (3%)
  local copies, waits for them, and re-layouts  4.91 us (1%)
    all_gather x1, waiting for transfers between devices, local(): weights = lax.all_gather(conv_weight, 'phase', axis=0, tiled=True)  67.4 us
    all_gather x3, blocking collectives, whole_of(): filled = lax.all_gather(filled, axes[number], axis=dim, tiled=True)  52.2 us
    ppermute x9, waiting for transfers between devices, padded_2(): before = lax.ppermute(last, axis, up)  36.4 us
    ppermute x9, starting transfers between devices, padded_2(): before = lax.ppermute(last, axis, up)  31.9 us
    all_gather x1, waiting for transfers between devices, whole_of(): filled = lax.all_gather(filled, axes[number], axis=dim, tiled=True)  31.9 us
    all_to_all x1, waiting for transfers between devices, copy_for_each(): lax.all_to_all(jnp.broadcast_to(value[None], (devices, *value.shape)), ax...  29.8 us
    ppermute x9, starting transfers between devices, padded_2(): after = lax.ppermute(first, axis, down)  25.1 us
    dot_general x8, matrix products, image_layer(): jnp.einsum('ok,fkp->fop', weight, stacked, preferred_element_type=jnp.flo...  16.7 us
  transfers between devices with their start and end apart: 21, of which 12 were waited for; matrix products, arithmetic and copies ran while one was open for 0% of the time, Pallas kernels for 0%

commit v1 on v0

--- a/solution.py
+++ b/solution.py
@@ -102,7 +102,8 @@
     phase_now = lax.axis_index("phase")
     phases = lax.axis_size("phase")
     own_frames = point_feats.shape[0]
-    weights = lax.all_gather(conv_weight, "phase", axis=0, tiled=True)
+    copies = jnp.concatenate([conv_weight] * lax.axis_size("phase"), axis=0)
+    weights = lax.all_to_all(copies, "phase", 0, 0, tiled=True)
     start_maps = lax.dynamic_slice_in_dim(image, phase_now * own_frames, own_frames, 0)
 
     def layer_step(layer, activation):

time: 345 us -> 397 us (1.15)
  waiting for transfers between devices: 168 us -> 204 us
  starting transfers between devices: 62.5 us -> 73 us
  local copies, waits for them, and re-layouts: 4.91 us -> 9.71 us
    all_to_all x0 -> x1, waiting for transfers between devices: none -> 106 us  [local(): weights = lax.all_to_all(copies, 'phase', 0, 0, tiled=True)]
    all_gather x1 -> x0, waiting for transfers between devices: 67.4 us -> none  [local(): weights = lax.all_gather(conv_weight, 'phase', axis=0, tiled=True)]
    concatenate x0 -> x1, local copies, waits for them, and re-layouts: none -> 5.66 us  [local(): copies = jnp.concatenate([conv_weight] * lax.axis_size('phase'), axis=0)]
    ppermute x9, starting transfers between devices: 25.1 us -> 30.6 us  [padded_2(): after = lax.ppermute(first, axis, down)]
    all_to_all x0 -> x1, starting transfers between devices: none -> 5.06 us  [local(): weights = lax.all_to_all(copies, 'phase', 0, 0, tiled=True)]
where the time goes in v1:
time: 397 us; the launch traced here: 395 us
  waiting for transfers between devices  204 us (51%)
  starting transfers between devices  73 us (18%)
  blocking collectives  51.9 us (13%)
  matrix products  31 us (8%)
  between operations  14.3 us (4%)
  other arithmetic  10.2 us (3%)
  local copies, waits for them, and re-layouts  9.71 us (2%)
    all_to_all x1, waiting for transfers between devices, local(): weights = lax.all_to_all(copies, 'phase', 0, 0, tiled=True)  106 us
    all_gather x3, blocking collectives, whole_of(): filled = lax.all_gather(filled, axes[number], axis=dim, tiled=True)  51.9 us
    ppermute x9, waiting for transfers between devices, padded_2(): before = lax.ppermute(last, axis, up)  36.4 us
    ppermute x9, starting transfers between devices, padded_2(): before = lax.ppermute(last, axis, up)  31.9 us
    all_gather x1, waiting for transfers between devices, whole_of(): filled = lax.all_gather(filled, axes[number], axis=dim, tiled=True)  31 us
    ppermute x9, starting transfers between devices, padded_2(): after = lax.ppermute(first, axis, down)  30.6 us
    all_to_all x1, waiting for transfers between devices, copy_for_each(): lax.all_to_all(jnp.broadcast_to(value[None], (devices, *value.shape)), ax...  29.3 us
    dot_general x8, matrix products, image_layer(): jnp.einsum('ok,fkp->fop', weight, stacked, preferred_element_type=jnp.flo...  16.7 us
  transfers between devices with their start and end apart: 21, of which 12 were waited for; matrix products, arithmetic and copies ran while one was open for 0% of the time, Pallas kernels for 0%

profile of v1, /device:TPU:6, one launch (start us, length us, event | category | flops | bytes accessed | tf_op | source)
XLA Modules:
  0.0 395.3 jit_solution(6255621969345528638)
XLA Ops:
  7.2 5.7 %concatenate.86 = bf16[8,256,2304]{2,1,0:T(8,128)(2,1)} broadcast(bf16[256,2304]{1,0:T(8,128)(2,1)} %bitcast.76), dimensions={1,2} | broadcast | bytes 10616832 | tf_op jit(solution)/shard_map/concatenate | solution.py:105
  12.8 5.1 %all-to-all-start = ((bf16[8,256,2304]{2,1,0:T(8,128)(2,1)}), bf16[8,256,2304]{2,1,0:T(8,128)(2,1)}, u32[]{:S(2)}, u32[]{:S(2)}) async-start(bf16[8,256,2304]{2,1,0:T(8,128)(2,1)} %concatenate.86), calls=%async_computation | async-start | bytes 18874368 | tf_op jit(solution)/shard_map/all_to_all | solution.py:106
  18.1 105.6 %all-to-all-done = bf16[8,256,2304]{2,1,0:T(8,128)(2,1)} async-done(((bf16[8,256,2304]{2,1,0:T(8,128)(2,1)}), bf16[8,256,2304]{2,1,0:T(8,128)(2,1)}, u32[]{:S(2)}, u32[]{:S(2)}) %all-to-all-start) | async-done | bytes 9437216 | tf_op jit(solution)/shard_map/all_to_all | solution.py:106
  123.7 118.3 %while.18 = (s32[]{:T(128)}, bf16[2,256,256]{1,2,0:T(8,128)(2,1)S(1)}, bf16[8,256,2304]{2,1,0:T(8,128)(2,1)}, s32[]{:T(128)}) while((s32[]{:T(128)}, bf16[2,256,256]{1,2,0:T(8,128)(2,1)S(1)}, bf16[8,256,2304]{2,1,0:T(8,128)(2,1)}, s32[]{:T(128)}) %tuple.72), condition=%wide.region_1.2_spmd, body=%wide.region_0.1_spmd.sunk | while | flops 608062720 | bytes 11410577 | solution.py:112
  123.7 11.7 %collective-permute-start = (bf16[2,256,64]{1,2,0:T(8,128)(2,1)S(1)}, bf16[2,256,64]{1,2,0:T(8,128)(2,1)S(1)}, u32[]{:S(2)}, u32[]{:S(2)}) collective-permute-start(bf16[2,256,64]{1,2,0:T(8,128)(2,1)S(1)} %get-tuple-element.195), channel_id=1, source_target_pairs={{1,0},{2,1},{3,2},{4,3},{5,4},{6,5},{7,6},{8,7},{9,8},{10,9},{11,1... | collective-permute-start | bytes 196616 | tf_op jit(solution)/shard_map/while/body/eval_jaxpr/ppermute | solution.py:23
  137.4 6.3 %collective-permute-done.1 = bf16[2,256,64]{1,2,0:T(8,128)(2,1)S(1)} collective-permute-done((bf16[2,256,64]{1,2,0:T(8,128)(2,1)S(1)}, bf16[2,256,64]{1,2,0:T(8,128)(2,1)S(1)}, u32[]{:S(2)}, u32[]{:S(2)}) %collective-permute-start.1) | collective-permute-done | bytes 65568 | tf_op jit(solution)/shard_map/while/body/eval_jaxpr/ppermute | solution.py:22
  149.0 3.9 collective-permute-start.1
  153.0 4.3 %collective-permute-done.1 = bf16[2,256,64]{1,2,0:T(8,128)(2,1)S(1)} collective-permute-done((bf16[2,256,64]{1,2,0:T(8,128)(2,1)S(1)}, bf16[2,256,64]{1,2,0:T(8,128)(2,1)S(1)}, u32[]{:S(2)}, u32[]{:S(2)}) %collective-permute-start.1) | collective-permute-done | bytes 65568 | tf_op jit(solution)/shard_map/while/body/eval_jaxpr/ppermute | solution.py:22
  162.6 3.9 collective-permute-start.1
  166.5 4.3 %collective-permute-done.1 = bf16[2,256,64]{1,2,0:T(8,128)(2,1)S(1)} collective-permute-done((bf16[2,256,64]{1,2,0:T(8,128)(2,1)S(1)}, bf16[2,256,64]{1,2,0:T(8,128)(2,1)S(1)}, u32[]{:S(2)}, u32[]{:S(2)}) %collective-permute-start.1) | collective-permute-done | bytes 65568 | tf_op jit(solution)/shard_map/while/body/eval_jaxpr/ppermute | solution.py:22
  176.1 3.9 collective-permute-start.1
  180.1 4.3 %collective-permute-done.1 = bf16[2,256,64]{1,2,0:T(8,128)(2,1)S(1)} collective-permute-done((bf16[2,256,64]{1,2,0:T(8,128)(2,1)S(1)}, bf16[2,256,64]{1,2,0:T(8,128)(2,1)S(1)}, u32[]{:S(2)}, u32[]{:S(2)}) %collective-permute-start.1) | collective-permute-done | bytes 65568 | tf_op jit(solution)/shard_map/while/body/eval_jaxpr/ppermute | solution.py:22
  189.7 3.9 collective-permute-start.1
  193.7 4.3 %collective-permute-done.1 = bf16[2,256,64]{1,2,0:T(8,128)(2,1)S(1)} collective-permute-done((bf16[2,256,64]{1,2,0:T(8,128)(2,1)S(1)}, bf16[2,256,64]{1,2,0:T(8,128)(2,1)S(1)}, u32[]{:S(2)}, u32[]{:S(2)}) %collective-permute-start.1) | collective-permute-done | bytes 65568 | tf_op jit(solution)/shard_map/while/body/eval_jaxpr/ppermute | solution.py:22
  199.2 2.1 fusion.91
  203.3 3.9 collective-permute-start.1
  207.2 4.3 %collective-permute-done.1 = bf16[2,256,64]{1,2,0:T(8,128)(2,1)S(1)} collective-permute-done((bf16[2,256,64]{1,2,0:T(8,128)(2,1)S(1)}, bf16[2,256,64]{1,2,0:T(8,128)(2,1)S(1)}, u32[]{:S(2)}, u32[]{:S(2)}) %collective-permute-start.1) | collective-permute-done | bytes 65568 | tf_op jit(solution)/shard_map/while/body/eval_jaxpr/ppermute | solution.py:22
  216.8 3.9 collective-permute-start.1
  220.8 4.3 %collective-permute-done.1 = bf16[2,256,64]{1,2,0:T(8,128)(2,1)S(1)} collective-permute-done((bf16[2,256,64]{1,2,0:T(8,128)(2,1)S(1)}, bf16[2,256,64]{1,2,0:T(8,128)(2,1)S(1)}, u32[]{:S(2)}, u32[]{:S(2)}) %collective-permute-start.1) | collective-permute-done | bytes 65568 | tf_op jit(solution)/shard_map/while/body/eval_jaxpr/ppermute | solution.py:22
  230.4 3.9 collective-permute-start.1
  234.4 4.3 %collective-permute-done.1 = bf16[2,256,64]{1,2,0:T(8,128)(2,1)S(1)} collective-permute-done((bf16[2,256,64]{1,2,0:T(8,128)(2,1)S(1)}, bf16[2,256,64]{1,2,0:T(8,128)(2,1)S(1)}, u32[]{:S(2)}, u32[]{:S(2)}) %collective-permute-start.1) | collective-permute-done | bytes 65568 | tf_op jit(solution)/shard_map/while/body/eval_jaxpr/ppermute | solution.py:22
  239.9 2.1 fusion.91
  244.1 5.4 %all-to-all-start.1 = ((bf16[64,2,11,256]{3,1,2,0:T(2,128)(2,1)}), bf16[64,2,11,256]{3,1,2,0:T(2,128)(2,1)S(1)}, u32[]{:S(2)}, u32[]{:S(2)}) async-start(bf16[64,2,11,256]{3,1,2,0:T(2,128)(2,1)} %broadcast_in_dim.201), calls=%async_computation.1 | async-start | bytes 1441792 | tf_op jit(solution)/shard_map/all_to_all | solution.py:36
  249.6 29.3 %all-to-all-done.1 = bf16[64,2,11,256]{3,1,2,0:T(2,128)(2,1)S(1)} async-done(((bf16[64,2,11,256]{3,1,2,0:T(2,128)(2,1)}), bf16[64,2,11,256]{3,1,2,0:T(2,128)(2,1)S(1)}, u32[]{:S(2)}, u32[]{:S(2)}) %all-to-all-start.1) | async-done | bytes 720928 | tf_op jit(solution)/shard_map/all_to_all | solution.py:36
  280.6 6.5 %fusion.35 = f32[2,11,256]{2,1,0:T(8,128)S(1)} fusion(bf16[2,11,16384]{2,1,0:T(8,128)(2,1)} %reshape.133, s32[2,256]{1,0:T(2,128)S(1)} %copy-done.7), kind=kOutput, calls=%fused_computation.59 | convolution fusion | flops 192954880 | bytes 745472 | tf_op jit(solution)/shard_map/fkn,fnp->fkp/dot_general | solution.py:120
  287.5 13.0 %all_gather.14 = bf16[2,64,1024]{2,1,0:T(8,128)(2,1)} all-gather(bf16[2,64,256]{2,1,0:T(8,128)(2,1)S(1)} %fusion.30), channel_id=1, replica_groups=mesh['phase'=8,'wide_0'=4,'wide_1'=16] {'wide_0'}, dimensions={2}, use_global_device_ids=true | all-gather | bytes 327680 | tf_op jit(solution)/shard_map/all_gather | solution.py:48
  300.5 10.2 %all-gather = s32[2,1024]{1,0:T(2,128)S(1)} all-gather(s32[2,256]{1,0:T(2,128)S(1)} %copy-done.4), channel_id=2, replica_groups=mesh['phase'=8,'wide_0'=4,'wide_1'=16] {'wide_0'}, dimensions={1}, use_global_device_ids=true | all-gather | bytes 10240 | tf_op jit(solution)/shard_map/all_gather | solution.py:48
  310.7 28.7 %all-gather.1 = s32[2,16384]{1,0:T(2,128)S(1)} all-gather(s32[2,1024]{1,0:T(2,128)S(1)} %all-gather), channel_id=3, replica_groups=mesh['phase'=8,'wide_0'=4,'wide_1'=16] {'wide_1'}, dimensions={1}, use_global_device_ids=true | all-gather | bytes 139264 | tf_op jit(solution)/shard_map/all_gather | solution.py:48
  339.5 31.0 %all-gather.4.cloned.1.call-done = bf16[2,64,16384]{2,1,0:T(8,128)(2,1)} async-done(((bf16[2,64,1024]{2,1,0:T(8,128)(2,1)}), bf16[2,64,16384]{2,1,0:T(8,128)(2,1)}) %all-gather.4.cloned.1.call-update) | async-done | bytes 4194320 | tf_op jit(solution)/shard_map/all_gather | solution.py:48
  370.5 6.7 %fusion.31 = bf16[2,128,64]{1,2,0:T(8,128)(2,1)S(1)} fusion(bf16[2,64,16384]{2,1,0:T(8,128)(2,1)} %all-gather.4.cloned.1.call-done, s32[2,16384]{1,0:T(2,128)S(1)} %broadcast_subtract_fusion), kind=kOutput, calls=%fused_computation.55 | convolution fusion | flops 541081600 | bytes 4358144 | tf_op jit(solution)/shard_map/fjp,fpc->cfj/dot_general | solution.py:135
  377.3 2.5 collective-permute-start.2
  379.8 5.5 %collective-permute-start.3 = (bf16[128,128]{0,1:T(8,128)(2,1)S(1)}, bf16[128,128]{0,1:T(8,128)(2,1)S(1)}, u32[]{:S(2)}, u32[]{:S(2)}) collective-permute-start(bf16[128,128]{0,1:T(8,128)(2,1)S(1)} %bitcast.79), channel_id=1, source_target_pairs={{1,0},{2,1},{3,2},{4,3},{5,4},{6,5},{7,6},{8,7},{9,8},{10,9},{11,1... | collective-permute-start | bytes 98312 | tf_op jit(solution)/shard_map/ppermute | solution.py:23
  (205 shorter events, 44.7 us)
Async XLA Ops:
  7.2 10.8 %copy-start = (bf16[16,256,256]{2,1,0:T(8,128)(2,1)S(1)}, bf16[16,256,256]{2,1,0:T(8,128)(2,1)}, u32[]{:S(2)}) copy-start(bf16[16,256,256]{2,1,0:T(8,128)(2,1)} %param.12) | copy-start | bytes 6291460
  12.8 110.9 %all-to-all-start = ((bf16[8,256,2304]{2,1,0:T(8,128)(2,1)}), bf16[8,256,2304]{2,1,0:T(8,128)(2,1)}, u32[]{:S(2)}, u32[]{:S(2)}) async-start(bf16[8,256,2304]{2,1,0:T(8,128)(2,1)} %concatenate.86), calls=%async_computation | async-start | bytes 18874368 | tf_op jit(solution)/shard_map/all_to_all | solution.py:106
  123.7 118.3 %copy-start.3 = (bf16[11,256]{1,0:T(8,128)(2,1)S(1)}, bf16[11,256]{1,0:T(8,128)(2,1)}, u32[]{:S(2)}) copy-start(bf16[11,256]{1,0:T(8,128)(2,1)} %param.14) | copy-start | bytes 16900
  123.7 20.0 %collective-permute-start = (bf16[2,256,64]{1,2,0:T(8,128)(2,1)S(1)}, bf16[2,256,64]{1,2,0:T(8,128)(2,1)S(1)}, u32[]{:S(2)}, u32[]{:S(2)}) collective-permute-start(bf16[2,256,64]{1,2,0:T(8,128)(2,1)S(1)} %get-tuple-element.195), channel_id=1, source_target_pairs={{1,0},{2,1},{3,2},{4,3},{5,4},{6,5},{7,6},{8,7},{9,8},{10,9},{11,1... | collective-permute-start | bytes 196616 | tf_op jit(solution)/shard_map/while/body/eval_jaxpr/ppermute | solution.py:23
  135.4 8.3 %collective-permute-start.1 = (bf16[2,256,64]{1,2,0:T(8,128)(2,1)S(1)}, bf16[2,256,64]{1,2,0:T(8,128)(2,1)S(1)}, u32[]{:S(2)}, u32[]{:S(2)}) collective-permute-start(bf16[2,256,64]{1,2,0:T(8,128)(2,1)S(1)} %get-tuple-element.196), channel_id=1, source_target_pairs={{0,1},{1,2},{2,3},{3,4},{4,5},{5,6},{6,7},{7,8},{8,9},{9,10},{10,1... | collective-permute-start | bytes 196616 | tf_op jit(solution)/shard_map/while/body/eval_jaxpr/ppermute | solution.py:22
  147.1 10.2 %collective-permute-start = (bf16[2,256,64]{1,2,0:T(8,128)(2,1)S(1)}, bf16[2,256,64]{1,2,0:T(8,128)(2,1)S(1)}, u32[]{:S(2)}, u32[]{:S(2)}) collective-permute-start(bf16[2,256,64]{1,2,0:T(8,128)(2,1)S(1)} %get-tuple-element.195), channel_id=1, source_target_pairs={{1,0},{2,1},{3,2},{4,3},{5,4},{6,5},{7,6},{8,7},{9,8},{10,9},{11,1... | collective-permute-start | bytes 196616 | tf_op jit(solution)/shard_map/while/body/eval_jaxpr/ppermute | solution.py:23
  149.0 8.3 %collective-permute-start.1 = (bf16[2,256,64]{1,2,0:T(8,128)(2,1)S(1)}, bf16[2,256,64]{1,2,0:T(8,128)(2,1)S(1)}, u32[]{:S(2)}, u32[]{:S(2)}) collective-permute-start(bf16[2,256,64]{1,2,0:T(8,128)(2,1)S(1)} %get-tuple-element.196), channel_id=1, source_target_pairs={{0,1},{1,2},{2,3},{3,4},{4,5},{5,6},{6,7},{7,8},{8,9},{9,10},{10,1... | collective-permute-start | bytes 196616 | tf_op jit(solution)/shard_map/while/body/eval_jaxpr/ppermute | solution.py:22
  160.6 10.2 %collective-permute-start = (bf16[2,256,64]{1,2,0:T(8,128)(2,1)S(1)}, bf16[2,256,64]{1,2,0:T(8,128)(2,1)S(1)}, u32[]{:S(2)}, u32[]{:S(2)}) collective-permute-start(bf16[2,256,64]{1,2,0:T(8,128)(2,1)S(1)} %get-tuple-element.195), channel_id=1, source_target_pairs={{1,0},{2,1},{3,2},{4,3},{5,4},{6,5},{7,6},{8,7},{9,8},{10,9},{11,1... | collective-permute-start | bytes 196616 | tf_op jit(solution)/shard_map/while/body/eval_jaxpr/ppermute | solution.py:23
  162.6 8.3 %collective-permute-start.1 = (bf16[2,256,64]{1,2,0:T(8,128)(2,1)S(1)}, bf16[2,256,64]{1,2,0:T(8,128)(2,1)S(1)}, u32[]{:S(2)}, u32[]{:S(2)}) collective-permute-start(bf16[2,256,64]{1,2,0:T(8,128)(2,1)S(1)} %get-tuple-element.196), channel_id=1, source_target_pairs={{0,1},{1,2},{2,3},{3,4},{4,5},{5,6},{6,7},{7,8},{8,9},{9,10},{10,1... | collective-permute-start | bytes 196616 | tf_op jit(solution)/shard_map/while/body/eval_jaxpr/ppermute | solution.py:22
  174.2 10.2 %collective-permute-start = (bf16[2,256,64]{1,2,0:T(8,128)(2,1)S(1)}, bf16[2,256,64]{1,2,0:T(8,128)(2,1)S(1)}, u32[]{:S(2)}, u32[]{:S(2)}) collective-permute-start(bf16[2,256,64]{1,2,0:T(8,128)(2,1)S(1)} %get-tuple-element.195), channel_id=1, source_target_pairs={{1,0},{2,1},{3,2},{4,3},{5,4},{6,5},{7,6},{8,7},{9,8},{10,9},{11,1... | collective-permute-start | bytes 196616 | tf_op jit(solution)/shard_map/while/body/eval_jaxpr/ppermute | solution.py:23
  176.1 8.3 %collective-permute-start.1 = (bf16[2,256,64]{1,2,0:T(8,128)(2,1)S(1)}, bf16[2,256,64]{1,2,0:T(8,128)(2,1)S(1)}, u32[]{:S(2)}, u32[]{:S(2)}) collective-permute-start(bf16[2,256,64]{1,2,0:T(8,128)(2,1)S(1)} %get-tuple-element.196), channel_id=1, source_target_pairs={{0,1},{1,2},{2,3},{3,4},{4,5},{5,6},{6,7},{7,8},{8,9},{9,10},{10,1... | collective-permute-start | bytes 196616 | tf_op jit(solution)/shard_map/while/body/eval_jaxpr/ppermute | solution.py:22
  187.8 10.2 %collective-permute-start = (bf16[2,256,64]{1,2,0:T(8,128)(2,1)S(1)}, bf16[2,256,64]{1,2,0:T(8,128)(2,1)S(1)}, u32[]{:S(2)}, u32[]{:S(2)}) collective-permute-start(bf16[2,256,64]{1,2,0:T(8,128)(2,1)S(1)} %get-tuple-element.195), channel_id=1, source_target_pairs={{1,0},{2,1},{3,2},{4,3},{5,4},{6,5},{7,6},{8,7},{9,8},{10,9},{11,1... | collective-permute-start | bytes 196616 | tf_op jit(solution)/shard_map/while/body/eval_jaxpr/ppermute | solution.py:23
  189.7 8.3 %collective-permute-start.1 = (bf16[2,256,64]{1,2,0:T(8,128)(2,1)S(1)}, bf16[2,256,64]{1,2,0:T(8,128)(2,1)S(1)}, u32[]{:S(2)}, u32[]{:S(2)}) collective-permute-start(bf16[2,256,64]{1,2,0:T(8,128)(2,1)S(1)} %get-tuple-element.196), channel_id=1, source_target_pairs={{0,1},{1,2},{2,3},{3,4},{4,5},{5,6},{6,7},{7,8},{8,9},{9,10},{10,1... | collective-permute-start | bytes 196616 | tf_op jit(solution)/shard_map/while/body/eval_jaxpr/ppermute | solution.py:22
  201.3 10.2 %collective-permute-start = (bf16[2,256,64]{1,2,0:T(8,128)(2,1)S(1)}, bf16[2,256,64]{1,2,0:T(8,128)(2,1)S(1)}, u32[]{:S(2)}, u32[]{:S(2)}) collective-permute-start(bf16[2,256,64]{1,2,0:T(8,128)(2,1)S(1)} %get-tuple-element.195), channel_id=1, source_target_pairs={{1,0},{2,1},{3,2},{4,3},{5,4},{6,5},{7,6},{8,7},{9,8},{10,9},{11,1... | collective-permute-start | bytes 196616 | tf_op jit(solution)/shard_map/while/body/eval_jaxpr/ppermute | solution.py:23
  203.3 8.3 %collective-permute-start.1 = (bf16[2,256,64]{1,2,0:T(8,128)(2,1)S(1)}, bf16[2,256,64]{1,2,0:T(8,128)(2,1)S(1)}, u32[]{:S(2)}, u32[]{:S(2)}) collective-permute-start(bf16[2,256,64]{1,2,0:T(8,128)(2,1)S(1)} %get-tuple-element.196), channel_id=1, source_target_pairs={{0,1},{1,2},{2,3},{3,4},{4,5},{5,6},{6,7},{7,8},{8,9},{9,10},{10,1... | collective-permute-start | bytes 196616 | tf_op jit(solution)/shard_map/while/body/eval_jaxpr/ppermute | solution.py:22
  214.9 10.2 %collective-permute-start = (bf16[2,256,64]{1,2,0:T(8,128)(2,1)S(1)}, bf16[2,256,64]{1,2,0:T(8,128)(2,1)S(1)}, u32[]{:S(2)}, u32[]{:S(2)}) collective-permute-start(bf16[2,256,64]{1,2,0:T(8,128)(2,1)S(1)} %get-tuple-element.195), channel_id=1, source_target_pairs={{1,0},{2,1},{3,2},{4,3},{5,4},{6,5},{7,6},{8,7},{9,8},{10,9},{11,1... | collective-permute-start | bytes 196616 | tf_op jit(solution)/shard_map/while/body/eval_jaxpr/ppermute | solution.py:23
  216.8 8.3 %collective-permute-start.1 = (bf16[2,256,64]{1,2,0:T(8,128)(2,1)S(1)}, bf16[2,256,64]{1,2,0:T(8,128)(2,1)S(1)}, u32[]{:S(2)}, u32[]{:S(2)}) collective-permute-start(bf16[2,256,64]{1,2,0:T(8,128)(2,1)S(1)} %get-tuple-element.196), channel_id=1, source_target_pairs={{0,1},{1,2},{2,3},{3,4},{4,5},{5,6},{6,7},{7,8},{8,9},{9,10},{10,1... | collective-permute-start | bytes 196616 | tf_op jit(solution)/shard_map/while/body/eval_jaxpr/ppermute | solution.py:22
  228.5 10.2 %collective-permute-start = (bf16[2,256,64]{1,2,0:T(8,128)(2,1)S(1)}, bf16[2,256,64]{1,2,0:T(8,128)(2,1)S(1)}, u32[]{:S(2)}, u32[]{:S(2)}) collective-permute-start(bf16[2,256,64]{1,2,0:T(8,128)(2,1)S(1)} %get-tuple-element.195), channel_id=1, source_target_pairs={{1,0},{2,1},{3,2},{4,3},{5,4},{6,5},{7,6},{8,7},{9,8},{10,9},{11,1... | collective-permute-start | bytes 196616 | tf_op jit(solution)/shard_map/while/body/eval_jaxpr/ppermute | solution.py:23
  230.4 8.3 %collective-permute-start.1 = (bf16[2,256,64]{1,2,0:T(8,128)(2,1)S(1)}, bf16[2,256,64]{1,2,0:T(8,128)(2,1)S(1)}, u32[]{:S(2)}, u32[]{:S(2)}) collective-permute-start(bf16[2,256,64]{1,2,0:T(8,128)(2,1)S(1)} %get-tuple-element.196), channel_id=1, source_target_pairs={{0,1},{1,2},{2,3},{3,4},{4,5},{5,6},{6,7},{7,8},{8,9},{9,10},{10,1... | collective-permute-start | bytes 196616 | tf_op jit(solution)/shard_map/while/body/eval_jaxpr/ppermute | solution.py:22
  242.0 7.5 %copy-start.8 = (s32[2,1]{0,1:T(1,128)S(1)}, s32[2,1]{0,1:T(1,128)}, u32[]{:S(2)}) copy-start(s32[2,1]{0,1:T(1,128)} %param.18) | copy-start | bytes 28
  244.1 36.5 %copy-start.7 = (s32[2,256]{1,0:T(2,128)S(1)}, s32[2,256]{1,0:T(2,128)}, u32[]{:S(2)}) copy-start(s32[2,256]{1,0:T(2,128)} %param.16) | copy-start | bytes 6148
  244.1 34.9 %all-to-all-start.1 = ((bf16[64,2,11,256]{3,1,2,0:T(2,128)(2,1)}), bf16[64,2,11,256]{3,1,2,0:T(2,128)(2,1)S(1)}, u32[]{:S(2)}, u32[]{:S(2)}) async-start(bf16[64,2,11,256]{3,1,2,0:T(2,128)(2,1)} %broadcast_in_dim.201), calls=%async_computation.1 | async-start | bytes 1441792 | tf_op jit(solution)/shard_map/all_to_all | solution.py:36
  249.5 121.0 %all-gather.4.cloned.1.call-start = ((), (), s32[]{:S(2)}) async-start(), calls=%async_computation.2 | async-start | bytes 4456448 | tf_op jit(solution)/shard_map/all_gather | solution.py:48
  280.6 6.6 %copy-start.5 = (f32[2,4,256]{2,1,0:T(4,128)S(1)}, f32[2,4,256]{2,1,0:T(4,128)}, u32[]{:S(2)}) copy-start(f32[2,4,256]{2,1,0:T(4,128)} %param.15) | copy-start | bytes 24580
  280.6 6.6 %copy-start.6 = (f32[64,15]{0,1:T(8,128)S(1)}, f32[64,15]{0,1:T(8,128)}, u32[]{:S(2)}) copy-start(f32[64,15]{0,1:T(8,128)} %param.19) | copy-start | bytes 11524
  280.6 19.9 %copy-start.4 = (s32[2,256]{1,0:T(2,128)S(1)}, s32[2,256]{1,0:T(2,128)}, u32[]{:S(2)}) copy-start(s32[2,256]{1,0:T(2,128)} %param.17) | copy-start | bytes 6148
  339.5 47.8 %copy-start.1 = (bf16[576,384]{1,0:T(8,128)(2,1)S(1)}, bf16[576,384]{1,0:T(8,128)(2,1)}, u32[]{:S(2)}) copy-start(bf16[576,384]{1,0:T(8,128)(2,1)} %param.20) | copy-start | bytes 1327108
  339.5 47.8 %copy-start.2 = (bf16[384,20]{0,1:T(8,128)(2,1)S(1)}, bf16[384,20]{0,1:T(8,128)(2,1)}, u32[]{:S(2)}) copy-start(bf16[384,20]{0,1:T(8,128)(2,1)} %param.21) | copy-start | bytes 46084
  377.3 8.0 %collective-permute-start.2 = (bf16[128,128]{0,1:T(8,128)(2,1)S(1)}, bf16[128,128]{0,1:T(8,128)(2,1)S(1)}, u32[]{:S(2)}, u32[]{:S(2)}) collective-permute-start(bf16[128,128]{0,1:T(8,128)(2,1)S(1)} %bitcast.78), channel_id=1, source_target_pairs={{0,1},{1,2},{2,3},{3,4},{4,5},{5,6},{6,7},{7,8},{8,9},{9,10},{10,1... | collective-permute-start | bytes 98312 | tf_op jit(solution)/shard_map/ppermute | solution.py:22
  379.8 7.0 %collective-permute-start.3 = (bf16[128,128]{0,1:T(8,128)(2,1)S(1)}, bf16[128,128]{0,1:T(8,128)(2,1)S(1)}, u32[]{:S(2)}, u32[]{:S(2)}) collective-permute-start(bf16[128,128]{0,1:T(8,128)(2,1)S(1)} %bitcast.79), channel_id=1, source_target_pairs={{1,0},{2,1},{3,2},{4,3},{5,4},{6,5},{7,6},{8,7},{9,8},{10,9},{11,1... | collective-permute-start | bytes 98312 | tf_op jit(solution)/shard_map/ppermute | solution.py:23
Sparse Core Ops, SparseCore 0:
  300.6 69.8 all-gather.3
